TPU v7x, 32 devices: a whole 2x2x4 slice. The times are simulated.
32 devices in a mesh: dp: 4 (over y, core), tensor: 8 (over z, x).
Axes of the slice: x: 2, y: 2, z: 4, core: 2. Of those that a mesh axis runs over, the one named last changes fastest.
Arguments:
- ref_hidden: bfloat16 [1152, 4608], P('dp', 'tensor'), may hold values from -6 to 6
- pol_hidden: bfloat16 [1152, 4608], P('dp', 'tensor'), may hold values from -6 to 6
- readout: bfloat16 [1152, 4608], P('dp', 'tensor'), may hold values from -0.019897461 to 0.019897461
- lengths: int32 [12], P('dp'), may hold values from 16 to 96, as said below
- pairing: int32 [12], replicated, may hold values from 0 to 11, each once
- pre_gain: float32 [4608], replicated, may hold values from 0.25 to 1.75
- post_gain: float32 [4608], replicated, may hold values from 0.25 to 1.75
- w_query: bfloat16 [4608, 4096], P('dp', 'tensor'), may hold values from -0.09375 to 0.09375
- w_key: bfloat16 [4608, 2048], P('dp', 'tensor'), may hold values from -3 to 3
- value_projection: bfloat16 [4608, 2048], P('dp', 'tensor'), may hold values from -0.09375 to 0.09375
- w_out: bfloat16 [4608, 4096], P('dp', 'tensor'), may hold values from -0.09375 to 0.09375
- a_query: bfloat16 [4608, 64], P('dp'), may hold values from -0.09375 to 0.09375
- a_value: bfloat16 [4608, 64], P('dp'), may hold values from -0.09375 to 0.09375
- query_second_factor: bfloat16 [64, 4096], P(None, 'tensor'), may hold values from -0.75 to 0.75
- value_second_factor: bfloat16 [64, 2048], P(None, 'tensor'), may hold values from -0.75 to 0.75
Outputs:
- policy_out: bfloat16 [1152, 4608], P('dp', 'tensor')
- reference_out: bfloat16 [1152, 4608], P('dp', 'tensor')
- dpo_loss: float32 [], replicated
- grad_hidden: bfloat16 [1152, 4608], P('dp', 'tensor')
- grad_a: float32 [4608, 128], P('dp')
- query_factor_gradient: float32 [64, 4096], P(None, 'tensor')
- value_factor_gradient: float32 [64, 2048], P(None, 'tensor')
Inputs may be any that keep to these rules, and one draw needn't show every extreme that they name: `lengths`: every sequence has at least one valid token and some sequence is full. `pairing`: entries 2k and 2k + 1 name the chosen and the rejected sequence of pair k; every sequence appears once.
All inputs are finite; a program needn't handle non-finite values.
Results may differ from a plain program's by a relative error of at most 0.0233.
The roundings to bfloat16 on the way count: a program that leaves them out, or rounds other values in their place, can miss the bound.
Values may be sent and summed in bfloat16 or wider, within the bound.
A program may use at most 128 MiB of HBM per device.

v0:
```python
import jax
import jax.numpy as jnp
from jax import lax
from jax.sharding import PartitionSpec as P

MODEL_WIDTH = 4608
HQ = 32
HEAD_SIZE = 128
NORM_EPS = 1e-06
SOFT_CAP = 50.0
ADAPTER_SCALE = 0.5
DPO_BETA = 0.5
LOSS_SCALE = 256.0
ROPE_BASE = 10000.0


def query_scale():
    return float(MODEL_WIDTH // HQ) ** (-0.5)


def apply_rotation(value_rows, direction):
    length = value_rows.shape[1]
    head_depth = value_rows.shape[3]
    middle = head_depth // 2
    spacing = ROPE_BASE ** (-2.0 * jnp.arange(middle, dtype=jnp.float32) / head_depth)
    angles = jnp.arange(length, dtype=jnp.float32)[:, None] * spacing[None, :]
    cosine = jnp.cos(angles)[None, :, None, :]
    sine_part = direction * jnp.sin(angles)[None, :, None, :]
    leading = value_rows[..., :middle]
    trailing = value_rows[..., middle:]
    return jnp.concatenate(
        [leading * cosine - trailing * sine_part, trailing * cosine + leading * sine_part], axis=-1
    )


def allowed_mask(lengths, length):
    places = jnp.arange(length)
    causal = places[None, :] <= places[:, None]
    living = places[None, :] < lengths[:, None]
    return causal[None, None, None, :, :] & living[:, None, None, None, :]


def attend(query_rows, rotated_keys, value_rows, lengths):
    seqs_here, length, q_heads, head_depth = query_rows.shape
    kv_heads = rotated_keys.shape[2]
    grouped_heads = query_rows.reshape(seqs_here, length, kv_heads, q_heads // kv_heads, head_depth)
    scores = (
        jnp.einsum(
            "sqkgd,spkd->skgqp", grouped_heads, rotated_keys, preferred_element_type=jnp.float32
        )
        * query_scale()
    )
    capped = SOFT_CAP * jnp.tanh(scores / SOFT_CAP)
    allowed = allowed_mask(lengths, length)
    weights = jnp.where(allowed, jnp.exp(capped), 0.0)
    probabilities = weights / jnp.sum(weights, axis=-1, keepdims=True)
    probs_low = probabilities.astype(jnp.bfloat16)
    mixed_out = jnp.einsum(
        "skgqp,spkd->sqkgd", probs_low, value_rows, preferred_element_type=jnp.float32
    )
    return (
        mixed_out.astype(jnp.bfloat16).reshape(seqs_here, length, q_heads, head_depth),
        probs_low,
        probabilities,
        capped,
    )


def attend_back(grad_mixed, query_rows, rotated_keys, value_rows, probs_low, probabilities, capped):
    seqs_here, length, q_heads, head_depth = query_rows.shape
    kv_heads = rotated_keys.shape[2]
    shape_five = (seqs_here, length, kv_heads, q_heads // kv_heads, head_depth)
    grouped_heads = query_rows.reshape(shape_five)
    grad_grouped = grad_mixed.reshape(shape_five)
    grad_probs = jnp.einsum(
        "sqkgd,spkd->skgqp", grad_grouped, value_rows, preferred_element_type=jnp.float32
    )
    value_rows_gradient = jnp.einsum(
        "skgqp,sqkgd->spkd", probs_low, grad_grouped, preferred_element_type=jnp.float32
    )
    centered = grad_probs - jnp.sum(grad_probs * probabilities, axis=-1, keepdims=True)
    grad_scores = (
        probabilities * centered * (1.0 - (capped / SOFT_CAP) ** 2) * query_scale()
    ).astype(jnp.bfloat16)
    query_rows_gradient = jnp.einsum(
        "skgqp,spkd->sqkgd", grad_scores, rotated_keys, preferred_element_type=jnp.float32
    ).reshape(seqs_here, length, q_heads, head_depth)
    key_rows_gradient = jnp.einsum(
        "skgqp,sqkgd->spkd", grad_scores, grouped_heads, preferred_element_type=jnp.float32
    )
    return (query_rows_gradient, key_rows_gradient, value_rows_gradient)


def normalize(hidden, pre_gain):
    whole_rows = lax.all_gather(hidden, "tensor", axis=1, tiled=True)
    wide_rows = whole_rows.astype(jnp.float32)
    pre_scale = lax.rsqrt(
        jnp.sum(wide_rows * wide_rows, axis=1, keepdims=True) / pre_gain.shape[0] + NORM_EPS
    )
    normed = (wide_rows * pre_scale * pre_gain).astype(jnp.bfloat16)
    return (normed, pre_scale)


def attention_layer(hidden, normed, weights, adapters, lengths, post_local):
    w_query, w_key, value_projection, w_out, a_query, a_value = weights
    tok_rows, full_width = normed.shape
    seqs_here = lengths.shape[0]
    length = tok_rows // seqs_here
    query_rows = jnp.dot(normed, w_query, preferred_element_type=jnp.float32)
    keys_before_rotation = jnp.dot(normed, w_key, preferred_element_type=jnp.float32)
    value_rows = jnp.dot(normed, value_projection, preferred_element_type=jnp.float32)
    low_rank_update = None
    if adapters is not None:
        query_second_factor, value_second_factor = adapters
        rank_size = query_second_factor.shape[0]
        low_rank_update = jnp.dot(
            normed, jnp.concatenate([a_query, a_value], axis=1), preferred_element_type=jnp.float32
        ).astype(jnp.bfloat16)
        query_rows = query_rows + ADAPTER_SCALE * jnp.dot(
            low_rank_update[:, :rank_size], query_second_factor, preferred_element_type=jnp.float32
        )
        value_rows = value_rows + ADAPTER_SCALE * jnp.dot(
            low_rank_update[:, rank_size:], value_second_factor, preferred_element_type=jnp.float32
        )
    q_heads = query_rows.shape[1] // HEAD_SIZE
    kv_heads = keys_before_rotation.shape[1] // HEAD_SIZE
    query_rows = apply_rotation(
        query_rows.reshape(seqs_here, length, q_heads, HEAD_SIZE), 1.0
    ).astype(jnp.bfloat16)
    rotated_keys = apply_rotation(
        keys_before_rotation.reshape(seqs_here, length, kv_heads, HEAD_SIZE), 1.0
    ).astype(jnp.bfloat16)
    value_rows = value_rows.reshape(seqs_here, length, kv_heads, HEAD_SIZE).astype(jnp.bfloat16)
    mixed_out, probs_low, probabilities, capped = attend(
        query_rows, rotated_keys, value_rows, lengths
    )
    head_terms = lax.dot_general(
        mixed_out.reshape(tok_rows, q_heads * HEAD_SIZE),
        w_out,
        (((1,), (1,)), ((), ())),
        preferred_element_type=jnp.float32,
    )
    summed = lax.psum_scatter(
        head_terms.astype(jnp.bfloat16), "tensor", scatter_dimension=1, tiled=True
    ).astype(jnp.float32)
    squares = lax.psum(jnp.sum(summed * summed, axis=1), "tensor")
    post_scale = lax.rsqrt(squares[:, None] / full_width + NORM_EPS)
    result = hidden.astype(jnp.float32) + summed * post_scale * post_local
    saved = (
        low_rank_update,
        query_rows,
        rotated_keys,
        value_rows,
        probs_low,
        probabilities,
        capped,
        summed,
        post_scale,
    )
    return (result, saved)


def body(
    ref_hidden,
    pol_hidden,
    readout,
    lengths,
    pairing,
    pre_gain,
    post_gain,
    w_query,
    w_key,
    value_projection,
    w_out,
    a_query,
    a_value,
    query_second_factor,
    value_second_factor,
):
    tok_rows, part_width = pol_hidden.shape
    seqs_here = lengths.shape[0]
    length = tok_rows // seqs_here
    tensor_rank = lax.axis_index("tensor")
    data_rank = lax.axis_index("dp")
    all_seqs = seqs_here * lax.axis_size("dp")
    full_width = part_width * lax.axis_size("tensor")
    pre_local = lax.dynamic_slice_in_dim(pre_gain, tensor_rank * part_width, part_width)
    post_local = lax.dynamic_slice_in_dim(post_gain, tensor_rank * part_width, part_width)
    weights = (
        lax.all_gather(w_query, "dp", axis=0, tiled=True),
        lax.all_gather(w_key, "dp", axis=0, tiled=True),
        lax.all_gather(value_projection, "dp", axis=0, tiled=True),
        lax.all_gather(w_out, "dp", axis=0, tiled=True),
        lax.all_gather(a_query, "dp", axis=0, tiled=True),
        lax.all_gather(a_value, "dp", axis=0, tiled=True),
    )
    w_query_all, w_key_all, w_value_all, w_out_all, a_query_all, a_value_all = weights
    ref_normed, ref_scale = normalize(ref_hidden, pre_gain)
    ref_result, ref_saved = attention_layer(
        ref_hidden, ref_normed, weights, None, lengths, post_local
    )
    pol_normed, pol_scale = normalize(pol_hidden, pre_gain)
    pol_result, pol_saved = attention_layer(
        pol_hidden,
        pol_normed,
        weights,
        (query_second_factor, value_second_factor),
        lengths,
        post_local,
    )
    readout_wide = readout.astype(jnp.float32)
    living = (jnp.arange(length)[None, :] < lengths[:, None]).astype(jnp.float32)

    def sequence_score(result):
        return jnp.sum(
            jnp.sum(result * readout_wide, axis=1).reshape(seqs_here, length) * living, axis=1
        )

    placed = jnp.zeros((2, all_seqs), jnp.float32)
    offset = data_rank * seqs_here
    placed = lax.dynamic_update_slice(
        placed,
        jnp.stack([sequence_score(ref_result), sequence_score(pol_result)]),
        (jnp.int32(0), offset),
    )
    scores = lax.psum(placed, ("dp", "tensor"))
    ratios = scores[1] - scores[0]
    chooser = (pairing[:, None] == jnp.arange(all_seqs)[None, :]).astype(jnp.float32)
    picked = jnp.dot(chooser, ratios, precision=lax.Precision.HIGHEST).reshape(-1, 2)
    margins = DPO_BETA * (picked[:, 0] - picked[:, 1])
    dpo_loss = jnp.sum(jax.nn.softplus(-margins))
    pair_pull = DPO_BETA * LOSS_SCALE * jax.nn.sigmoid(-margins)
    signed = jnp.stack([-pair_pull, pair_pull], axis=1).reshape(-1)
    coefficients = jnp.dot(signed, chooser, precision=lax.Precision.HIGHEST)
    local_coef = lax.dynamic_slice_in_dim(coefficients, offset, seqs_here)
    grad_result = (local_coef[:, None] * living).reshape(tok_rows, 1) * readout_wide
    (
        low_rank_update,
        query_rows,
        rotated_keys,
        value_rows,
        probs_low,
        probabilities,
        capped,
        summed,
        post_scale,
    ) = pol_saved
    post_dot = lax.psum(jnp.sum(summed * post_local * grad_result, axis=1), "tensor")
    grad_summed = (
        post_scale * post_local * grad_result
        - summed * post_scale**3 * post_dot[:, None] / full_width
    )
    grad_wide = lax.all_gather(grad_summed.astype(jnp.bfloat16), "tensor", axis=1, tiled=True)
    grad_mixed = jnp.dot(grad_wide, w_out_all, preferred_element_type=jnp.float32).astype(
        jnp.bfloat16
    )
    q_heads = query_rows.shape[2]
    grad_q_rot, rotated_key_gradient, value_head_gradient = attend_back(
        grad_mixed.reshape(seqs_here, length, q_heads, HEAD_SIZE),
        query_rows,
        rotated_keys,
        value_rows,
        probs_low,
        probabilities,
        capped,
    )
    query_rows_gradient = (
        apply_rotation(grad_q_rot, -1.0).reshape(tok_rows, -1).astype(jnp.bfloat16)
    )
    key_rows_gradient = (
        apply_rotation(rotated_key_gradient, -1.0).reshape(tok_rows, -1).astype(jnp.bfloat16)
    )
    value_rows_gradient = value_head_gradient.reshape(tok_rows, -1).astype(jnp.bfloat16)
    rank_size = query_second_factor.shape[0]
    rows_contraction = (((0,), (0,)), ((), ()))
    contract_cols = (((1,), (1,)), ((), ()))
    query_adapter_term = ADAPTER_SCALE * lax.dot_general(
        low_rank_update[:, :rank_size],
        query_rows_gradient,
        rows_contraction,
        preferred_element_type=jnp.float32,
    )
    value_adapter_term = ADAPTER_SCALE * lax.dot_general(
        low_rank_update[:, rank_size:],
        value_rows_gradient,
        rows_contraction,
        preferred_element_type=jnp.float32,
    )
    query_factor_gradient, value_factor_gradient = (
        lax.psum(query_adapter_term.astype(jnp.bfloat16), "dp").astype(jnp.float32),
        lax.psum(value_adapter_term.astype(jnp.bfloat16), "dp").astype(jnp.float32),
    )
    adapter_grad = jnp.concatenate(
        [
            ADAPTER_SCALE
            * lax.dot_general(
                query_rows_gradient,
                query_second_factor,
                contract_cols,
                preferred_element_type=jnp.float32,
            ),
            ADAPTER_SCALE
            * lax.dot_general(
                value_rows_gradient,
                value_second_factor,
                contract_cols,
                preferred_element_type=jnp.float32,
            ),
        ],
        axis=1,
    ).astype(jnp.bfloat16)
    adapter_term = lax.dot_general(
        pol_normed, adapter_grad, rows_contraction, preferred_element_type=jnp.float32
    )
    adapter_part = lax.psum_scatter(
        adapter_term.astype(jnp.bfloat16), "dp", scatter_dimension=0, tiled=True
    )
    grad_a = lax.psum(adapter_part, "tensor").astype(jnp.float32)
    a_both = jnp.concatenate([a_query_all, a_value_all], axis=1)
    input_terms = lax.dot_general(
        query_rows_gradient, w_query_all, contract_cols, preferred_element_type=jnp.float32
    )
    input_terms = input_terms + lax.dot_general(
        key_rows_gradient, w_key_all, contract_cols, preferred_element_type=jnp.float32
    )
    input_terms = input_terms + lax.dot_general(
        value_rows_gradient, w_value_all, contract_cols, preferred_element_type=jnp.float32
    )
    input_terms = input_terms + lax.dot_general(
        adapter_grad, a_both, contract_cols, preferred_element_type=jnp.float32
    )
    input_whole = lax.psum(input_terms.astype(jnp.bfloat16), "tensor").astype(jnp.float32)
    grad_normed = lax.dynamic_slice_in_dim(input_whole, tensor_rank * part_width, part_width, 1)
    narrow = pol_hidden.astype(jnp.float32)
    pre_dot = lax.psum(jnp.sum(narrow * pre_local * grad_normed, axis=1), "tensor")
    grad_hidden = (
        grad_result
        + pol_scale * pre_local * grad_normed
        - narrow * pol_scale**3 * pre_dot[:, None] / full_width
    )
    return (
        pol_result.astype(jnp.bfloat16),
        ref_result.astype(jnp.bfloat16),
        dpo_loss,
        grad_hidden.astype(jnp.bfloat16),
        grad_a,
        query_factor_gradient,
        value_factor_gradient,
    )


def solution(mesh):
    placed = (
        P("dp", "tensor"),
        P("dp", "tensor"),
        P("dp", "tensor"),
        P("dp"),
        P(),
        P(),
        P(),
        P("dp", "tensor"),
        P("dp", "tensor"),
        P("dp", "tensor"),
        P("dp", "tensor"),
        P("dp", None),
        P("dp", None),
        P(None, "tensor"),
        P(None, "tensor"),
    )
    return jax.shard_map(
        body,
        mesh=mesh,
        in_specs=placed,
        out_specs=(
            P("dp", "tensor"),
            P("dp", "tensor"),
            P(),
            P("dp", "tensor"),
            P("dp", None),
            P(None, "tensor"),
            P(None, "tensor"),
        ),
        check_vma=False,
    )
```

profile of v0, /device:TPU:0, one launch (start us, length us, event | category | flops | bytes accessed | tf_op | source)
XLA Modules:
  0.0 823.5 jit_solution(8016594998505936199)
XLA Ops:
  11.2 9.0 %all_gather.29 = bf16[4608,64]{0,1:T(8,128)(2,1)S(1)} all-gather(bf16[1152,64]{0,1:T(8,128)(2,1)S(1)} %copy-done.29), channel_id=1, replica_groups=mesh['dp'=4,'tensor'=8] {'dp'}, dimensions={0}, use_global_device_ids=true | all-gather | bytes 737280 | tf_op jit(solution)/shard_map/all_gather | solution.py:194
  20.3 7.6 all_gather.30
  29.8 41.2 %all-gather.21.cloned.1.call-done = bf16[8,576,288]{1,2,0:T(8,128)(2,1)} async-done(((bf16[1,576,288]{1,2,0:T(8,128)(2,1)}), bf16[8,576,288]{1,2,0:T(8,128)(2,1)}) %all-gather.21.cloned.1.call-update) | async-done | bytes 2654224 | tf_op jit(solution)/shard_map/all_gather | solution.py:95
  71.0 5.3 copy.72
  76.4 7.2 reshape.270
  83.6 46.3 %all-gather.19.cloned.1.call-done = bf16[8,576,288]{1,2,0:T(8,128)(2,1)} async-done(((bf16[1,576,288]{1,2,0:T(8,128)(2,1)}), bf16[8,576,288]{1,2,0:T(8,128)(2,1)}) %all-gather.19.cloned.1.call-update) | async-done | bytes 2654224 | tf_op jit(solution)/shard_map/all_gather | solution.py:95
  129.8 5.3 copy.64
  135.2 7.8 reshape.269
  162.0 17.6 %all-gather.11.cloned.1.call-done = bf16[4608,256]{1,0:T(8,128)(2,1)} async-done(((bf16[1152,256]{1,0:T(8,128)(2,1)}), bf16[4608,256]{1,0:T(8,128)(2,1)}) %all-gather.11.cloned.1.call-update) | async-done | bytes 2359312 | tf_op jit(solution)/shard_map/all_gather | solution.py:192
  186.1 32.4 %all-gather.15.cloned.1.call-done = bf16[4608,512]{1,0:T(8,128)(2,1)} async-done(((bf16[1152,512]{1,0:T(8,128)(2,1)}), bf16[4608,512]{1,0:T(8,128)(2,1)}) %all-gather.15.cloned.1.call-update) | async-done | bytes 4718608 | tf_op jit(solution)/shard_map/all_gather | solution.py:190
  218.5 5.5 fusion.142
  225.2 4.4 fusion.140
  239.0 18.4 %all-gather.17.cloned.1.call-done = bf16[4608,512]{1,0:T(8,128)(2,1)} async-done(((bf16[1152,512]{1,0:T(8,128)(2,1)}), bf16[4608,512]{1,0:T(8,128)(2,1)}) %all-gather.17.cloned.1.call-update) | async-done | bytes 4718608 | tf_op jit(solution)/shard_map/all_gather | solution.py:193
  257.4 5.4 convolution_convert_fusion
  262.8 4.7 copy.110
  276.2 5.6 convolution_convert_fusion.1
  281.8 4.7 copy.108
  288.0 59.2 %reduce-scatter.12.cloned.1.call-done = bf16[576,288]{1,0:T(8,128)(2,1)} async-done(((bf16[4608,288]{1,0:T(8,128)(2,1)}), bf16[576,288]{1,0:T(8,128)(2,1)}) %reduce-scatter.12.cloned.1.call-update) | async-done | bytes 331792
  349.1 80.8 %reduce-scatter.10.cloned.1.call-done = bf16[576,288]{1,0:T(8,128)(2,1)} async-done(((bf16[4608,288]{1,0:T(8,128)(2,1)}), bf16[576,288]{1,0:T(8,128)(2,1)}) %reduce-scatter.10.cloned.1.call-update) | async-done | bytes 331792
  432.4 20.1 %all-reduce = (f32[288]{0:T(512)S(1)}, f32[288]{0:T(512)S(1)}) all-reduce(f32[288]{0:T(512)S(1)} %fusion.45, f32[288]{0:T(512)S(1)} %fusion.32), channel_id=1, replica_groups=mesh['dp'=4,'tensor'=8] {'tensor'}, use_global_device_ids=true, to_apply=%region_4.5 | all-reduce | flops 576 | bytes 4608 | tf_op jit(solution)/shard_map/psum | solution.py:146
  457.0 36.8 %psum.65 = f32[2,12]{1,0:T(2,128)S(1)} all-reduce(f32[2,12]{1,0:T(2,128)S(1)} %dynamic_update_slice.3), channel_id=1, replica_groups=mesh['dp'=4,'tensor'=8] {'dp','tensor'}, use_global_device_ids=true, to_apply=%region_14.15 | all-reduce | flops 24 | bytes 192 | tf_op jit(solution)/shard_map/psum | solution.py:226
  496.8 21.1 %psum.66 = f32[288]{0:T(512)S(1)} all-reduce(f32[288]{0:T(512)S(1)} %fusion.38), channel_id=1, replica_groups=mesh['dp'=4,'tensor'=8] {'tensor'}, use_global_device_ids=true, to_apply=%region_17.18 | all-reduce | flops 288 | bytes 2304 | tf_op jit(solution)/shard_map/psum | solution.py:248
  519.2 55.1 %all-gather.23.cloned.1.call-done = bf16[8,576,288]{1,2,0:T(8,128)(2,1)} async-done(((bf16[1,576,288]{1,2,0:T(8,128)(2,1)}), bf16[8,576,288]{1,2,0:T(8,128)(2,1)}) %all-gather.23.cloned.1.call-update) | async-done | bytes 2654224 | tf_op jit(solution)/shard_map/all_gather | solution.py:253
  574.4 4.4 copy.82
  578.8 5.6 reshape.268
  584.4 5.4 convolution_convert_fusion.3
  609.0 4.3 fusion.58
  618.7 10.8 %reduce-scatter.8.cloned.1.call-done = bf16[1152,128]{1,0:T(8,128)(2,1)} async-done(((bf16[4608,128]{1,0:T(8,128)(2,1)}), bf16[1152,128]{1,0:T(8,128)(2,1)}) %reduce-scatter.8.cloned.1.call-update) | async-done | bytes 294928 | tf_op jit(solution)/shard_map/reduce_scatter | solution.py:315
  631.2 10.5 %psum.71 = bf16[64,256]{1,0:T(8,128)(2,1)S(1)} all-reduce(bf16[64,256]{1,0:T(8,128)(2,1)S(1)} %fusion.23), channel_id=1, replica_groups=mesh['dp'=4,'tensor'=8] {'dp'}, use_global_device_ids=true, to_apply=%region_25.26 | all-reduce | flops 16384 | bytes 65536 | tf_op jit(solution)/shard_map/psum | solution.py:291
  642.4 21.6 %all-reduce.5.cloned.1.call-done = bf16[64,512]{1,0:T(8,128)(2,1)} async-done(((bf16[64,512]{1,0:T(8,128)(2,1)}), bf16[64,512]{1,0:T(8,128)(2,1)}) %all-reduce.5.cloned.1.call-update) | async-done | bytes 65552 | tf_op jit(solution)/shard_map/psum | solution.py:290
  665.5 126.0 %all-reduce.7.cloned.1.call-done = (bf16[288,4608]{1,0:T(8,128)(2,1)}, bf16[1152,128]{1,0:T(8,128)(2,1)}) async-done(((bf16[288,4608]{1,0:T(8,128)(2,1)}, bf16[1152,128]{1,0:T(8,128)(2,1)}), (bf16[288,4608]{1,0:T(8,128)(2,1)}, bf16[1152,128]{1,0:T(8,128)(2,1)})) %all-reduce.7.cloned.1.call-update) | async-done | bytes 2949136 | tf_op jit(solution)/shard_map/psum | solution.py:332
  792.8 19.4 %psum.68 = f32[288]{0:T(512)S(1)} all-reduce(f32[288]{0:T(512)S(1)} %fusion.35), channel_id=1, replica_groups=mesh['dp'=4,'tensor'=8] {'tensor'}, use_global_device_ids=true, to_apply=%region_21.22 | all-reduce | flops 288 | bytes 2304 | tf_op jit(solution)/shard_map/psum | solution.py:335
  (211 shorter events, 98.8 us)
Async XLA Ops:
  7.2 222.5 %copy-start = (bf16[64,512]{1,0:T(8,128)(2,1)S(1)}, bf16[64,512]{1,0:T(8,128)(2,1)}, u32[]{:S(2)}) copy-start(bf16[64,512]{1,0:T(8,128)(2,1)} %param.28) | copy-start | bytes 196612
  7.2 63.8 %all-gather.21.cloned.1.call-start = ((), (), s32[]{:S(2)}) async-start(), calls=%async_computation.10 | async-start | bytes 3317760 | tf_op jit(solution)/shard_map/all_gather | solution.py:95
  7.9 121.9 %all-gather.19.cloned.1.call-start = ((), (), s32[]{:S(2)}) async-start(), calls=%async_computation.9 | async-start | bytes 3317760 | tf_op jit(solution)/shard_map/all_gather | solution.py:95
  8.7 11.6 %copy-start.30 = (bf16[1152,64]{0,1:T(8,128)(2,1)S(1)}, bf16[1152,64]{0,1:T(8,128)(2,1)}, u32[]{:S(2)}) copy-start(bf16[1152,64]{0,1:T(8,128)(2,1)} %param.27) | copy-start | bytes 442372
  8.7 145.4 %all-gather.13.cloned.1.call-start = ((), (), s32[]{:S(2)}) async-start(), calls=%async_computation.4 | async-start | bytes 2949120 | tf_op jit(solution)/shard_map/all_gather | solution.py:191
  9.4 170.2 %all-gather.11.cloned.1.call-start = ((), (), s32[]{:S(2)}) async-start(), calls=%async_computation.3 | async-start | bytes 2949120 | tf_op jit(solution)/shard_map/all_gather | solution.py:192
  10.0 18.0 %copy-start.40 = (s32[3]{0:T(128)S(1)}, s32[3]{0:T(128)}, u32[]{:S(2)}) copy-start(s32[3]{0:T(128)} %param.18) | copy-start | bytes 40
  10.0 208.5 %all-gather.15.cloned.1.call-start = ((), (), s32[]{:S(2)}) async-start(), calls=%async_computation.5 | async-start | bytes 5898240 | tf_op jit(solution)/shard_map/all_gather | solution.py:190
  10.6 246.8 %all-gather.17.cloned.1.call-start = ((), (), s32[]{:S(2)}) async-start(), calls=%async_computation.6 | async-start | bytes 5898240 | tf_op jit(solution)/shard_map/all_gather | solution.py:193
  11.2 336.0 %reduce-scatter.12.cloned.1.call-start = ((), (), s32[]{:S(2)}) async-start(), calls=%async_computation.13 | async-start | bytes 3981312
  28.1 48.3 %copy-start.3 = (bf16[4608,128]{0,1:T(8,128)(2,1)}, bf16[4608,128]{0,1:T(8,128)(2,1)S(1)}, u32[]{:S(2)}) copy-start(bf16[4608,128]{0,1:T(8,128)(2,1)S(1)} %constant_dynamic-update-slice_fusion) | copy-start | bytes 3538948
  29.8 203.0 %copy-start.12 = (f32[96,64]{1,0:T(8,128)}, f32[96,64]{1,0:T(8,128)S(1)}, u32[]{:S(2)}) copy-start(f32[96,64]{1,0:T(8,128)S(1)} %get-tuple-element.50) | copy-start | bytes 73732
  135.2 12.9 %copy-start.36 = (f32[4608]{0:T(1024)S(1)}, f32[4608]{0:T(1024)}, u32[]{:S(2)}) copy-start(f32[4608]{0:T(1024)} %param.20) | copy-start | bytes 55300
  148.1 4.9 copy-start.37
  267.6 4.6 copy-start.15
  267.6 4.7 copy-start.14
  267.6 162.2 %reduce-scatter.10.cloned.1.call-start = ((), (), s32[]{:S(2)}) async-start(), calls=%async_computation.12 | async-start | bytes 3981312
  286.5 166.0 %copy-start.6 = (bf16[288,576]{1,0:T(8,128)(2,1)S(1)}, bf16[288,576]{1,0:T(8,128)(2,1)}, u32[]{:S(2)}) copy-start(bf16[288,576]{1,0:T(8,128)(2,1)} %param.17) | copy-start | bytes 995332
  286.5 287.9 %all-gather.23.cloned.1.call-start = ((), (), s32[]{:S(2)}) async-start(), calls=%async_computation.11 | async-start | bytes 3317760 | tf_op jit(solution)/shard_map/all_gather | solution.py:253
  519.0 110.6 %reduce-scatter.8.cloned.1.call-start = ((), (), s32[]{:S(2)}) async-start(), calls=%async_computation.7 | async-start | bytes 1474560 | tf_op jit(solution)/shard_map/reduce_scatter | solution.py:315
  584.4 8.5 %copy-start.33 = (pred[3,96,96]{1,2,0:T(8,128)(4,1)S(1)}, pred[3,96,96]{1,2,0:T(8,128)(4,1)}, u32[]{:S(2)}) copy-start(pred[3,96,96]{1,2,0:T(8,128)(4,1)} %broadcast_and_fusion) | copy-start | bytes 82948
  584.4 8.5 %copy-start.45 = (f32[3,2,2,96]{3,2,1,0:T(2,128)S(1)}, f32[3,2,2,96]{3,2,1,0:T(2,128)}, u32[]{:S(2)}) copy-start(f32[3,2,2,96]{3,2,1,0:T(2,128)} %copy-done.44) | copy-start | bytes 13828
  595.0 4.8 copy-start.28
  595.0 5.6 copy-start.35
  595.0 5.8 copy-start.13
  595.0 5.8 copy-start.17
  605.1 58.9 %all-reduce.5.cloned.1.call-start = ((), (), s32[]{:S(2)}) async-start(), calls=%async_computation.8 | async-start | bytes 131072 | tf_op jit(solution)/shard_map/psum | solution.py:290
  609.0 182.5 %all-reduce.7.cloned.1.call-start = ((), (), s32[]{:S(2)}) async-start(), calls=%async_computation.14 | async-start | bytes 5898240 | tf_op jit(solution)/shard_map/psum | solution.py:332
  618.7 11.6 %copy-start.42 = (f32[6,1]{0,1:T(1,128)S(1)}, f32[6,1]{0,1:T(1,128)}, u32[]{:S(2)}) copy-start(f32[6,1]{0,1:T(1,128)} %get-tuple-element.17) | copy-start | bytes 76
  618.7 172.8 %copy-start.7 = (bf16[288,576]{1,0:T(8,128)(2,1)S(1)}, bf16[288,576]{1,0:T(8,128)(2,1)}, u32[]{:S(2)}) copy-start(bf16[288,576]{1,0:T(8,128)(2,1)} %param.16) | copy-start | bytes 995332
  618.7 195.4 %copy-start.38 = (f32[288]{0:T(512)S(1)}, f32[288]{0:T(512)}, u32[]{:S(2)}) copy-start(f32[288]{0:T(512)} %copy-done.37) | copy-start | bytes 3460
  618.7 195.4 %copy-start.39 = (f32[288]{0:T(512)S(1)}, f32[288]{0:T(512)}, u32[]{:S(2)}) copy-start(f32[288]{0:T(512)} %get-tuple-element.44) | copy-start | bytes 3460
  (26 other events, 55.9 us)
Sparse Core Ops, SparseCore 0:
  10.2 60.8 all-gather.20
  73.2 56.5 all-gather.18
  131.4 22.6 all-gather.12
  155.5 24.0 all-gather.10
  181.0 37.4 all-gather.14
  219.9 37.4 all-gather.16
  267.7 79.4 reduce-scatter.11
  350.8 79.0 reduce-scatter.9
  519.1 55.2 all-gather.22
  605.2 24.2 reduce-scatter.7
  632.4 31.5 all-reduce.4
  667.5 123.9 all-reduce.6
where the time goes:
time: 829 us; the launch traced here: 824 us
  waiting for transfers between devices  514 us (62%)
  blocking collectives  125 us (15%)
  matrix products  69.4 us (8%)
  local copies, waits for them, and re-layouts  68.9 us (8%)
  other arithmetic  30.4 us (4%)
  between operations  15.1 us (2%)
    unnamed x14, waiting for transfers between devices  144 us
    psum x1, waiting for transfers between devices, body(): lax.psum(input_terms.astype(jnp.bfloat16), 'tensor').astype(jnp.float32)  126 us
    all_gather x2, waiting for transfers between devices, normalize(): whole_rows = lax.all_gather(hidden, 'tensor', axis=1, tiled=True)  87.5 us
    all_gather x1, waiting for transfers between devices, body(): lax.all_gather(grad_summed.astype(jnp.bfloat16), 'tensor', axis=1, tiled=...  55.1 us
    psum x1, blocking collectives, body(): scores = lax.psum(placed, ('dp', 'tensor'))  36.8 us
    all_gather x1, waiting for transfers between devices, body(): lax.all_gather(w_query, 'dp', axis=0, tiled=True)  32.4 us
    convert_element_type x4, local copies, waits for them, and re-layouts, normalize(): wide_rows = whole_rows.astype(jnp.float32)  25.6 us
    unnamed x98, local copies, waits for them, and re-layouts  24.7 us
  transfers between devices with their start and end apart: 12, of which 12 were waited for; matrix products, arithmetic and copies ran while one was open for 13% of the time, Pallas kernels for 0%

commit v1 on v0

--- a/solution.py
+++ b/solution.py
@@ -329,7 +329,9 @@
     input_terms = input_terms + lax.dot_general(
         adapter_grad, a_both, contract_cols, preferred_element_type=jnp.float32
     )
-    input_whole = lax.psum(input_terms.astype(jnp.bfloat16), "tensor").astype(jnp.float32)
+    input_whole = jnp.sum(
+        lax.all_gather(input_terms.astype(jnp.bfloat16), "tensor"), axis=0
+    ).astype(jnp.float32)
     grad_normed = lax.dynamic_slice_in_dim(input_whole, tensor_rank * part_width, part_width, 1)
     narrow = pol_hidden.astype(jnp.float32)
     pre_dot = lax.psum(jnp.sum(narrow * pre_local * grad_normed, axis=1), "tensor")

time: 829 us -> 1190 us (1.44)
  waiting for transfers between devices: 514 us -> 862 us
    all_gather x0 -> x1, waiting for transfers between devices: none -> 405 us  [body(): lax.all_gather(input_terms.astype(jnp.bfloat16), 'tensor')]
    psum x1, waiting for transfers between devices: 126 us -> 73 us  [body(): grad_a = lax.psum(adapter_part, 'tensor').astype(jnp.float32)]
    unnamed x14 -> x15, waiting for transfers between devices: 144 us -> 143 us
  transfers between devices with their start and end apart: 12 -> 13, of which waited for: 12 -> 13; matrix products, arithmetic and copies ran while one was open for 13% -> 10% of each run, Pallas kernels for 0% -> 0%
where the time goes in v1:
time: 1190 us
  waiting for transfers between devices  862 us (72%)
  blocking collectives  126 us (11%)
  matrix products  74.3 us (6%)
  local copies, waits for them, and re-layouts  68.3 us (6%)
  other arithmetic  39.5 us (3%)
  between operations  14.8 us (1%)
    all_gather x1, waiting for transfers between devices, body(): lax.all_gather(input_terms.astype(jnp.bfloat16), 'tensor')  405 us
    unnamed x15, waiting for transfers between devices  143 us
    all_gather x2, waiting for transfers between devices, normalize(): whole_rows = lax.all_gather(hidden, 'tensor', axis=1, tiled=True)  87.5 us
    psum x1, waiting for transfers between devices, body(): grad_a = lax.psum(adapter_part, 'tensor').astype(jnp.float32)  73 us
    all_gather x1, waiting for transfers between devices, body(): lax.all_gather(grad_summed.astype(jnp.bfloat16), 'tensor', axis=1, tiled=...  55.2 us
    psum x1, blocking collectives, body(): scores = lax.psum(placed, ('dp', 'tensor'))  36.8 us
    all_gather x1, waiting for transfers between devices, body(): lax.all_gather(w_query, 'dp', axis=0, tiled=True)  32.4 us
    convert_element_type x4, local copies, waits for them, and re-layouts, normalize(): wide_rows = whole_rows.astype(jnp.float32)  25.4 us
  transfers between devices with their start and end apart: 13, of which 13 were waited for; matrix products, arithmetic and copies ran while one was open for 10% of the time, Pallas kernels for 0%

profile of v1, /device:TPU:0, one launch (start us, length us, event | category | flops | bytes accessed | tf_op | source)
XLA Modules:
  0.0 1185.6 jit_solution(11255086920662160387)
XLA Ops:
  11.2 9.0 all_gather.35
  20.3 7.6 all_gather.36
  29.8 41.2 %all-gather.25.cloned.1.call-done = bf16[8,576,288]{1,2,0:T(8,128)(2,1)} async-done(((bf16[1,576,288]{1,2,0:T(8,128)(2,1)}), bf16[8,576,288]{1,2,0:T(8,128)(2,1)}) %all-gather.25.cloned.1.call-update) | async-done | bytes 2654224 | tf_op jit(solution)/shard_map/all_gather | solution.py:95
  71.0 5.3 copy.72
  76.4 7.2 reshape.271
  83.6 46.3 %all-gather.23.cloned.1.call-done = bf16[8,576,288]{1,2,0:T(8,128)(2,1)} async-done(((bf16[1,576,288]{1,2,0:T(8,128)(2,1)}), bf16[8,576,288]{1,2,0:T(8,128)(2,1)}) %all-gather.23.cloned.1.call-update) | async-done | bytes 2654224 | tf_op jit(solution)/shard_map/all_gather | solution.py:95
  129.8 5.3 copy.64
  135.2 7.6 reshape.270
  162.0 17.6 %all-gather.13.cloned.1.call-done = bf16[4608,256]{1,0:T(8,128)(2,1)} async-done(((bf16[1152,256]{1,0:T(8,128)(2,1)}), bf16[4608,256]{1,0:T(8,128)(2,1)}) %all-gather.13.cloned.1.call-update) | async-done | bytes 2359312 | tf_op jit(solution)/shard_map/all_gather | solution.py:192
  186.1 32.4 %all-gather.17.cloned.1.call-done = bf16[4608,512]{1,0:T(8,128)(2,1)} async-done(((bf16[1152,512]{1,0:T(8,128)(2,1)}), bf16[4608,512]{1,0:T(8,128)(2,1)}) %all-gather.17.cloned.1.call-update) | async-done | bytes 4718608 | tf_op jit(solution)/shard_map/all_gather | solution.py:190
  218.5 5.5 fusion.142
  239.0 18.4 %all-gather.19.cloned.1.call-done = bf16[4608,512]{1,0:T(8,128)(2,1)} async-done(((bf16[1152,512]{1,0:T(8,128)(2,1)}), bf16[4608,512]{1,0:T(8,128)(2,1)}) %all-gather.19.cloned.1.call-update) | async-done | bytes 4718608 | tf_op jit(solution)/shard_map/all_gather | solution.py:193
  257.4 5.4 convolution_convert_fusion
  262.8 4.7 copy.110
  276.5 5.6 convolution_convert_fusion.1
  282.1 4.7 copy.108
  288.3 58.8 %reduce-scatter.12.cloned.1.call-done = bf16[576,288]{1,0:T(8,128)(2,1)} async-done(((bf16[4608,288]{1,0:T(8,128)(2,1)}), bf16[576,288]{1,0:T(8,128)(2,1)}) %reduce-scatter.12.cloned.1.call-update) | async-done | bytes 331792
  349.0 80.8 %reduce-scatter.10.cloned.1.call-done = bf16[576,288]{1,0:T(8,128)(2,1)} async-done(((bf16[4608,288]{1,0:T(8,128)(2,1)}), bf16[576,288]{1,0:T(8,128)(2,1)}) %reduce-scatter.10.cloned.1.call-update) | async-done | bytes 331792
  432.4 20.1 %all-reduce = (f32[288]{0:T(512)S(1)}, f32[288]{0:T(512)S(1)}) all-reduce(f32[288]{0:T(512)S(1)} %fusion.45, f32[288]{0:T(512)S(1)} %fusion.32), channel_id=1, replica_groups=mesh['dp'=4,'tensor'=8] {'tensor'}, use_global_device_ids=true, to_apply=%region_4.5 | all-reduce | flops 576 | bytes 4608 | tf_op jit(solution)/shard_map/psum | solution.py:146
  456.9 36.8 %psum.58 = f32[2,12]{1,0:T(2,128)S(1)} all-reduce(f32[2,12]{1,0:T(2,128)S(1)} %dynamic_update_slice.3), channel_id=1, replica_groups=mesh['dp'=4,'tensor'=8] {'dp','tensor'}, use_global_device_ids=true, to_apply=%region_14.15 | all-reduce | flops 24 | bytes 192 | tf_op jit(solution)/shard_map/psum | solution.py:226
  496.8 21.1 %psum.59 = f32[288]{0:T(512)S(1)} all-reduce(f32[288]{0:T(512)S(1)} %fusion.38), channel_id=1, replica_groups=mesh['dp'=4,'tensor'=8] {'tensor'}, use_global_device_ids=true, to_apply=%region_17.18 | all-reduce | flops 288 | bytes 2304 | tf_op jit(solution)/shard_map/psum | solution.py:248
  519.2 55.2 %all-gather.27.cloned.1.call-done = bf16[8,576,288]{1,2,0:T(8,128)(2,1)} async-done(((bf16[1,576,288]{1,2,0:T(8,128)(2,1)}), bf16[8,576,288]{1,2,0:T(8,128)(2,1)}) %all-gather.27.cloned.1.call-update) | async-done | bytes 2654224 | tf_op jit(solution)/shard_map/all_gather | solution.py:253
  578.7 5.7 reshape.269
  584.4 5.4 convolution_convert_fusion.3
  618.3 11.3 reduce-scatter.8.cloned.1.call-done
  629.7 4.9 fusion.1
  636.3 10.9 psum.63
  647.8 16.2 %all-reduce.6.cloned.1.call-done = bf16[64,512]{1,0:T(8,128)(2,1)} async-done(((bf16[64,512]{1,0:T(8,128)(2,1)}), bf16[64,512]{1,0:T(8,128)(2,1)}) %all-reduce.6.cloned.1.call-update) | async-done | bytes 65552 | tf_op jit(solution)/shard_map/psum | solution.py:290
  665.5 73.0 %all-reduce.4.cloned.1.call-done = bf16[1152,128]{1,0:T(8,128)(2,1)} async-done(((bf16[1152,128]{1,0:T(8,128)(2,1)}), bf16[1152,128]{1,0:T(8,128)(2,1)}) %all-reduce.4.cloned.1.call-update) | async-done | bytes 294928 | tf_op jit(solution)/shard_map/psum | solution.py:318
  740.4 405.4 %all-gather.21.cloned.1.call-done = bf16[2304,4608]{1,0:T(8,128)(2,1)} async-done(((bf16[288,4608]{1,0:T(8,128)(2,1)}), bf16[2304,4608]{1,0:T(8,128)(2,1)}) %all-gather.21.cloned.1.call-update) | async-done | bytes 21233680 | tf_op jit(solution)/shard_map/all_gather | solution.py:333
  1145.8 11.1 reduce_sum.151
  1157.3 20.2 %psum.60 = f32[288]{0:T(512)S(1)} all-reduce(f32[288]{0:T(512)S(1)} %fusion.35), channel_id=1, replica_groups=mesh['dp'=4,'tensor'=8] {'tensor'}, use_global_device_ids=true, to_apply=%region_21.22 | all-reduce | flops 288 | bytes 2304 | tf_op jit(solution)/shard_map/psum | solution.py:337
  (215 shorter events, 110.0 us)
Async XLA Ops:
  7.2 222.4 %copy-start = (bf16[64,512]{1,0:T(8,128)(2,1)S(1)}, bf16[64,512]{1,0:T(8,128)(2,1)}, u32[]{:S(2)}) copy-start(bf16[64,512]{1,0:T(8,128)(2,1)} %param.28) | copy-start | bytes 196612
  7.2 63.8 %all-gather.25.cloned.1.call-start = ((), (), s32[]{:S(2)}) async-start(), calls=%async_computation.12 | async-start | bytes 3317760 | tf_op jit(solution)/shard_map/all_gather | solution.py:95
  7.9 121.9 %all-gather.23.cloned.1.call-start = ((), (), s32[]{:S(2)}) async-start(), calls=%async_computation.11 | async-start | bytes 3317760 | tf_op jit(solution)/shard_map/all_gather | solution.py:95
  8.7 11.6 copy-start.30
  8.7 145.4 %all-gather.15.cloned.1.call-start = ((), (), s32[]{:S(2)}) async-start(), calls=%async_computation.4 | async-start | bytes 2949120 | tf_op jit(solution)/shard_map/all_gather | solution.py:191
  9.4 170.2 %all-gather.13.cloned.1.call-start = ((), (), s32[]{:S(2)}) async-start(), calls=%async_computation.3 | async-start | bytes 2949120 | tf_op jit(solution)/shard_map/all_gather | solution.py:192
  10.0 18.0 %copy-start.40 = (s32[3]{0:T(128)S(1)}, s32[3]{0:T(128)}, u32[]{:S(2)}) copy-start(s32[3]{0:T(128)} %param.18) | copy-start | bytes 40
  10.0 208.5 %all-gather.17.cloned.1.call-start = ((), (), s32[]{:S(2)}) async-start(), calls=%async_computation.5 | async-start | bytes 5898240 | tf_op jit(solution)/shard_map/all_gather | solution.py:190
  10.6 246.8 %all-gather.19.cloned.1.call-start = ((), (), s32[]{:S(2)}) async-start(), calls=%async_computation.6 | async-start | bytes 5898240 | tf_op jit(solution)/shard_map/all_gather | solution.py:193
  11.2 335.9 %reduce-scatter.12.cloned.1.call-start = ((), (), s32[]{:S(2)}) async-start(), calls=%async_computation.15 | async-start | bytes 3981312
  28.1 48.3 %copy-start.3 = (bf16[4608,128]{0,1:T(8,128)(2,1)}, bf16[4608,128]{0,1:T(8,128)(2,1)S(1)}, u32[]{:S(2)}) copy-start(bf16[4608,128]{0,1:T(8,128)(2,1)S(1)} %constant_dynamic-update-slice_fusion) | copy-start | bytes 3538948
  29.8 202.9 %copy-start.12 = (f32[96,64]{1,0:T(8,128)}, f32[96,64]{1,0:T(8,128)S(1)}, u32[]{:S(2)}) copy-start(f32[96,64]{1,0:T(8,128)S(1)} %get-tuple-element.48) | copy-start | bytes 73732
  135.2 12.8 %copy-start.36 = (f32[4608]{0:T(1024)S(1)}, f32[4608]{0:T(1024)}, u32[]{:S(2)}) copy-start(f32[4608]{0:T(1024)} %param.20) | copy-start | bytes 55300
  267.5 5.1 copy-start.14
  267.6 162.2 %reduce-scatter.10.cloned.1.call-start = ((), (), s32[]{:S(2)}) async-start(), calls=%async_computation.14 | async-start | bytes 3981312
  286.8 165.6 %copy-start.6 = (bf16[288,576]{1,0:T(8,128)(2,1)S(1)}, bf16[288,576]{1,0:T(8,128)(2,1)}, u32[]{:S(2)}) copy-start(bf16[288,576]{1,0:T(8,128)(2,1)} %param.17) | copy-start | bytes 995332
  286.9 287.5 %all-gather.27.cloned.1.call-start = ((), (), s32[]{:S(2)}) async-start(), calls=%async_computation.13 | async-start | bytes 3317760 | tf_op jit(solution)/shard_map/all_gather | solution.py:253
  518.9 110.6 %reduce-scatter.8.cloned.1.call-start = ((), (), s32[]{:S(2)}) async-start(), calls=%async_computation.7 | async-start | bytes 1474560 | tf_op jit(solution)/shard_map/reduce_scatter | solution.py:315
  584.4 8.5 copy-start.33
  584.4 8.5 copy-start.45
  595.0 5.6 copy-start.35
  595.0 5.8 copy-start.13
  595.0 5.8 copy-start.17
  605.1 58.9 %all-reduce.6.cloned.1.call-start = ((), (), s32[]{:S(2)}) async-start(), calls=%async_computation.9 | async-start | bytes 131072 | tf_op jit(solution)/shard_map/psum | solution.py:290
  609.0 129.5 %all-reduce.4.cloned.1.call-start = ((), (), s32[]{:S(2)}) async-start(), calls=%async_computation.8 | async-start | bytes 589824 | tf_op jit(solution)/shard_map/psum | solution.py:318
  615.0 14.6 %copy-start.5 = (bf16[4608,128]{0,1:T(8,128)(2,1)S(1)}, bf16[4608,128]{0,1:T(8,128)(2,1)}, u32[]{:S(2)}) copy-start(bf16[4608,128]{0,1:T(8,128)(2,1)} %copy-done.3) | copy-start | bytes 3538948
  615.0 14.6 %copy-start.22 = (bf16[288,64]{0,1:T(8,128)(2,1)S(1)}, bf16[288,64]{0,1:T(8,128)(2,1)}, u32[]{:S(2)}) copy-start(bf16[288,64]{0,1:T(8,128)(2,1)} %copy-done.21) | copy-start | bytes 110596
  615.0 14.6 %copy-start.24 = (bf16[288,64]{0,1:T(8,128)(2,1)S(1)}, bf16[288,64]{0,1:T(8,128)(2,1)}, u32[]{:S(2)}) copy-start(bf16[288,64]{0,1:T(8,128)(2,1)} %copy-done.23) | copy-start | bytes 110596
  629.6 516.2 %all-gather.21.cloned.1.call-start = ((), (), s32[]{:S(2)}) async-start(), calls=%async_computation.10 | async-start | bytes 23887872 | tf_op jit(solution)/shard_map/all_gather | solution.py:333
  1145.8 11.1 copy-start.7
  1145.8 31.7 %copy-start.38 = (f32[288]{0:T(512)S(1)}, f32[288]{0:T(512)}, u32[]{:S(2)}) copy-start(f32[288]{0:T(512)} %copy-done.37) | copy-start | bytes 3460
  1145.8 31.7 %copy-start.39 = (f32[288]{0:T(512)S(1)}, f32[288]{0:T(512)}, u32[]{:S(2)}) copy-start(f32[288]{0:T(512)} %get-tuple-element.42) | copy-start | bytes 3460
  (27 other events, 67.8 us)
Sparse Core Ops, SparseCore 0:
  10.2 60.8 all-gather.24
  73.2 56.5 all-gather.22
  131.4 22.6 all-gather.14
  155.5 24.0 all-gather.12
  181.0 37.4 all-gather.16
  219.9 37.4 all-gather.18
  267.6 79.4 reduce-scatter.11
  350.7 79.0 reduce-scatter.9
  519.1 55.2 all-gather.26
  605.2 24.2 reduce-scatter.7
  632.5 31.5 all-reduce.5
  667.2 71.3 all-reduce.3
  740.1 405.6 all-gather.20
